TPU v7x, 32 devices: a 4x4x1 block of a 4x4x8 slice. The times are simulated.
32 devices in a mesh: data: 1 (over z), dap2: 4 (over y), dap: 8 (over x, core).
Axes of the slice: x: 4, y: 4, z: 1, core: 2. Of those that a mesh axis runs over, the one named last changes fastest.
The devices are a block of a 4x4x8 slice.
Arguments:
- pair_rep: float32 [512, 512, 128], P(('data', 'dap2', 'dap'))
- pair_mask: int32 [512, 512], P(('data', 'dap2', 'dap'))
- norm_gain: bfloat16 [2, 128], replicated
- norm_bias: bfloat16 [2, 128], replicated
- w_proj: bfloat16 [2, 128, 512], replicated
- w_gate: bfloat16 [2, 128, 128], replicated
- post_gain: bfloat16 [2, 128], replicated
- post_bias: bfloat16 [2, 128], replicated
- w_out: bfloat16 [2, 128, 128], replicated
Outputs:
- output: float32 [512, 512, 128], P(('data', 'dap2', 'dap'))
All inputs are finite; a program needn't handle non-finite values.
Results may differ from a plain program's by a relative error of at most 0.00136737.
Values are sent between devices in bfloat16 or wider.
A program may use at most 768 MiB of HBM per device.

v0:
```python
import jax
import jax.numpy as jnp
from jax import lax
from jax.sharding import PartitionSpec as P

NORM_EPS = 1e-5
GROUP_AXES = ('dap2', 'dap')
ROW_SPEC = P(('data', 'dap2', 'dap'), None, None)
MASK_SPEC = P(('data', 'dap2', 'dap'), None)


def layer_norm(values, scale_vec, shift_vec, norm_axis):
    row_mean = jnp.mean(values, axis=norm_axis, keepdims=True)
    centered = values - row_mean
    row_var = jnp.mean(centered * centered, axis=norm_axis, keepdims=True)
    scaled = centered * lax.rsqrt(row_var + NORM_EPS)
    return (scaled * scale_vec.astype(jnp.float32) + shift_vec.astype(jnp.float32)).astype(jnp.bfloat16)


def gated_side(normed, w_pair, keep_mask, form):
    channels = w_pair.shape[1] // 2
    projected = jnp.einsum(form, normed, w_pair, preferred_element_type=jnp.float32)
    return (keep_mask * jax.nn.sigmoid(projected[channels:]) * projected[:channels]).astype(jnp.bfloat16)


def finish(pair_rows, normed, mixed_sum, post_gain, post_bias, w_gate, w_out):
    post_norm = layer_norm(mixed_sum, post_gain[:, None, None], post_bias[:, None, None], 0)
    update = jnp.einsum('cij,cd->ijd', post_norm, w_out, preferred_element_type=jnp.float32)
    gate_pre = jnp.einsum('ijd,de->ije', normed, w_gate, preferred_element_type=jnp.float32)
    return pair_rows + jax.nn.sigmoid(gate_pre) * update


def solution(mesh):
    def local_step(pair_rows, mask_rows, norm_gain, norm_bias, w_proj, w_gate, post_gain, post_bias, w_out):
        channels = w_out.shape[1]
        keep_mask = mask_rows.astype(jnp.float32)
        normed = layer_norm(pair_rows, norm_gain[0], norm_bias[0], -1)
        side_a = gated_side(normed, w_proj[0, :, :2 * channels], keep_mask, 'ikd,de->eik')
        side_b = gated_side(normed, w_proj[0, :, 2 * channels:], keep_mask, 'jkd,de->ejk')
        full_b = lax.all_gather(side_b, GROUP_AXES, axis=1, tiled=True)
        mixed_sum = jnp.einsum('cik,cjk->cij', side_a, full_b, preferred_element_type=jnp.float32)
        pair_mid = finish(pair_rows, normed, mixed_sum, post_gain[0], post_bias[0], w_gate[0], w_out[0])
        normed = layer_norm(pair_mid, norm_gain[1], norm_bias[1], -1)
        side_a = gated_side(normed, w_proj[1, :, :2 * channels], keep_mask, 'kid,de->eki')
        side_b = gated_side(normed, w_proj[1, :, 2 * channels:], keep_mask, 'kjd,de->ekj')
        cols_a = lax.all_to_all(side_a, GROUP_AXES, 2, 1, tiled=True)
        full_b = lax.all_gather(side_b, GROUP_AXES, axis=1, tiled=True)
        mixed_sum = jnp.einsum('cki,ckj->cij', cols_a, full_b, preferred_element_type=jnp.float32)
        return finish(pair_mid, normed, mixed_sum, post_gain[1], post_bias[1], w_gate[1], w_out[1])

    replicated = P()
    return jax.shard_map(local_step, mesh=mesh,
                         in_specs=(ROW_SPEC, MASK_SPEC) + (replicated,) * 7,
                         out_specs=ROW_SPEC, check_vma=False)
```

profile of v0, /device:TPU:97, one launch (start us, length us, event | category | flops | bytes accessed | tf_op | source)
XLA Modules:
  0.0 604.7 jit_solution(538862226523703799)
XLA Ops:
  6.6 3.4 reduce_sum.72
  9.9 4.2 multiply_reduce_fusion.3
  14.2 2.5 add_convert_fusion.3
  16.7 1.2 convolution_bitcast_fusion.2
  18.0 1.2 convolution_bitcast_fusion.3
  19.2 3.8 fusion.14
  23.0 4.0 copy.60
  27.6 5.3 copy.65
  33.0 4.7 copy.61
  37.7 2.7 fusion.35
  40.4 186.9 %all-gather.3.cloned.1.call-done = bf16[128,512,512]{2,0,1:T(8,128)(2,1)} async-done(((bf16[128,16,512]{2,0,1:T(8,128)(2,1)}), bf16[128,512,512]{2,0,1:T(8,128)(2,1)}) %all-gather.3.cloned.1.call-update) | async-done | bytes 67108880 | tf_op jit(solution)/shard_map/all_gather | solution.py:40
  227.3 56.7 %fusion.44 = (f32[16,512]{1,0:T(8,128)S(1)}, f32[128,16,512]{2,1,0:T(8,128)S(1)}) fusion(bf16[128,16,512]{2,1,0:T(8,128)(2,1)} %copy.61, bf16[128,512,512]{2,0,1:T(8,128)(2,1)} %all-gather.3.cloned.1.call-done), kind=kOutput, calls=%fused_computation.82 | convolution fusion | flops 1074782208 | bytes 73433088 | tf_op jit(solution)/shard_map/cik,cjk->cij/dot_general | solution.py:41
  285.2 1.0 copy-done.5
  286.2 1.4 copy-done.4
  287.6 3.3 fusion.45
  291.7 1.0 add_convert_fusion.1
  293.0 1.3 convolution_bitcast_fusion
  294.3 1.3 convolution_bitcast_fusion.1
  295.5 3.8 fusion.4
  299.4 3.9 copy.73
  303.3 4.3 copy.69
  307.6 3.8 all-to-all-start
  311.5 2.8 fusion.38
  314.3 44.5 %all-to-all-done = bf16[128,16,512]{0,1,2:T(8,128)(2,1)} async-done(((bf16[128,16,512]{0,1,2:T(8,128)(2,1)}), bf16[128,16,512]{0,1,2:T(8,128)(2,1)}, u32[]{:S(2)}, u32[]{:S(2)}) %all-to-all-start) | async-done | bytes 2097184 | tf_op jit(solution)/shard_map/all_to_all | solution.py:46
  358.8 3.5 copy.71
  362.3 3.9 copy.74
  366.2 153.0 %all-gather.5.cloned.1.call-done = bf16[128,512,512]{2,0,1:T(8,128)(2,1)} async-done(((bf16[128,16,512]{2,0,1:T(8,128)(2,1)}), bf16[128,512,512]{2,0,1:T(8,128)(2,1)}) %all-gather.5.cloned.1.call-update) | async-done | bytes 67108880 | tf_op jit(solution)/shard_map/all_gather | solution.py:47
  519.2 61.1 %fusion.46 = (f32[16,512]{1,0:T(8,128)S(1)}, f32[128,16,512]{2,1,0:T(8,128)}) fusion(bf16[128,512,16]{1,2,0:T(8,128)(2,1)S(1)} %copy.74, bf16[128,512,512]{2,0,1:T(8,128)(2,1)} %all-gather.5.cloned.1.call-done), kind=kOutput, calls=%fused_computation.84 | convolution fusion | flops 1074782208 | bytes 73433088 | tf_op jit(solution)/shard_map/cki,ckj->cij/dot_general | solution.py:48
  580.4 2.8 multiply_reduce_fusion
  584.5 1.1 copy-done.3
  585.6 6.5 %multiply_add_fusion = f32[16,512,128]{1,2,0:T(8,128)} fusion(f32[16,512,128]{1,2,0:T(8,128)S(1)} %copy-done.3, f32[16,512,128]{1,2,0:T(8,128)} %fusion.38, bf16[128,16,512]{2,1,0:T(8,128)(2,1)S(1)} %add_convert_fusion, bf16[2,128,128]{2,1,0:T(8,128)(2,1)S(1)} %copy-done.13), kind=kOutput, calls=%fused_computation.32 | convolution fusion | flops 273678336 | bytes 14712832 | tf_op jit(solution)/shard_map/cij,cd->ijd/dot_general | solution.py:28
  592.1 5.3 copy.78
  (44 shorter events, 4.2 us)
Async XLA Ops:
  6.5 7.6 %copy-start.10 = (bf16[2,128]{1,0:T(2,128)(2,1)S(1)}, bf16[2,128]{1,0:T(2,128)(2,1)}, u32[]{:S(2)}) copy-start(bf16[2,128]{1,0:T(2,128)(2,1)} %param.11) | copy-start | bytes 1540
  6.5 7.6 %copy-start.9 = (bf16[2,128]{1,0:T(2,128)(2,1)S(1)}, bf16[2,128]{1,0:T(2,128)(2,1)}, u32[]{:S(2)}) copy-start(bf16[2,128]{1,0:T(2,128)(2,1)} %param.12) | copy-start | bytes 1540
  6.6 220.8 %all-gather.3.cloned.1.call-start = ((), (), s32[]{:S(2)}) async-start(), calls=%async_computation.1 | async-start | bytes 69206016 | tf_op jit(solution)/shard_map/all_gather | solution.py:40
  9.9 4.3 copy-start
  14.1 2.6 copy-start.6
  17.9 1.2 copy-start.8
  27.0 492.2 %all-gather.5.cloned.1.call-start = ((), (), s32[]{:S(2)}) async-start(), calls=%async_computation.2 | async-start | bytes 69206016 | tf_op jit(solution)/shard_map/all_gather | solution.py:47
  33.0 4.7 copy-start.11
  33.0 4.7 copy-start.12
  33.0 4.7 copy-start.7
  284.0 2.2 copy-start.5
  284.5 3.1 copy-start.4
  284.5 3.1 copy-start.13
  291.0 2.0 copy-start.2
  307.6 51.2 %all-to-all-start = ((bf16[128,16,512]{0,1,2:T(8,128)(2,1)}), bf16[128,16,512]{0,1,2:T(8,128)(2,1)}, u32[]{:S(2)}, u32[]{:S(2)}) async-start(bf16[128,16,512]{0,1,2:T(8,128)(2,1)} %copy.69), calls=%async_computation | async-start | bytes 4194304 | tf_op jit(solution)/shard_map/all_to_all | solution.py:46
  580.4 3.5 copy-start.1
  583.2 2.3 copy-start.3
Sparse Core Ops, SparseCore 0:
  27.2 200.1 all-gather.2
  303.5 215.7 all-gather.4
where the time goes:
time: 610 us; the launch traced here: 605 us
  waiting for transfers between devices  385 us (63%)
  matrix products  138 us (23%)
  local copies, waits for them, and re-layouts  39.3 us (6%)
  other arithmetic  24 us (4%)
  between operations  14.2 us (2%)
    all_gather x2, waiting for transfers between devices, local_step(): full_b = lax.all_gather(side_b, GROUP_AXES, axis=1, tiled=True)  340 us
    dot_general x1, matrix products, local_step(): jnp.einsum('cki,ckj->cij', cols_a, full_b, preferred_element_type=jnp.flo...  61.1 us
    dot_general x1, matrix products, local_step(): jnp.einsum('cik,cjk->cij', side_a, full_b, preferred_element_type=jnp.flo...  56.7 us
    all_to_all x1, waiting for transfers between devices, local_step(): cols_a = lax.all_to_all(side_a, GROUP_AXES, 2, 1, tiled=True)  44.5 us
    convert_element_type x4, local copies, waits for them, and re-layouts, gated_side(): (keep_mask * jax.nn.sigmoid(projected[channels:]) * projected[:channels])...  16.8 us
  transfers between devices with their start and end apart: 3, of which 3 were waited for; matrix products, arithmetic and copies ran while one was open for 4% of the time, Pallas kernels for 0%

commit v1 on v0

v1 whole, which is shorter than its diff:
```python
import functools

import jax
import jax.numpy as jnp
from jax import lax
from jax.experimental import pallas as pl
from jax.experimental.pallas import tpu as pltpu
from jax.sharding import PartitionSpec as P

NORM_EPS = 1e-5
ROW_SPEC = P(('data', 'dap2', 'dap'), None, None)
MASK_SPEC = P(('data', 'dap2', 'dap'), None)
MESH = pl.DeviceIdType.MESH
F32, BF16 = jnp.float32, jnp.bfloat16
CORES = 2
LANES = 128
PAD = 8


def norm(values, gain, bias, axis):
    mean = jnp.mean(values, axis=axis, keepdims=True)
    centered = values - mean
    var = jnp.mean(centered * centered, axis=axis, keepdims=True)
    return (centered * lax.rsqrt(var + NORM_EPS) * gain + bias).astype(BF16)


def dot(a, b, ca, cb):
    return lax.dot_general(a, b, (((ca,), (cb,)), ((), ())), preferred_element_type=F32)


def update_kernel(ny, nx, incoming, z_ref, mask_ref, ng_ref, nb_ref, wp_ref, wg_ref, pg_ref, pb_ref, wo_ref, out_ref,
                  yn_ref, sa_ref, sb_ref, ab_ref, t_ref, r_ref, x_ref, u_ref, xr_ref,
                  p1s, p1r, p2s, p2r, x1s, x1r, x2s, x2r):
    rows, n, ch = z_ref.shape
    nt = n // LANES
    y = lax.axis_index('dap2')
    d = lax.axis_index('dap')
    x, c = d // CORES, d % CORES
    size1, size2 = (nx, ny), (ny, nx)
    pos1, pos2 = (x, y), (y, x)

    def peer(s, first, place, core):
        on_x = (s == 0) == first
        return {'dap2': y, 'dap': place * CORES + core} if on_x else {'dap2': place, 'dap': x * CORES + core}

    barrier = pltpu.get_barrier_semaphore()
    greeted = 0
    for on_x, size, pos in ((True, nx, x), (False, ny, y)):
        for o in range(size):
            for oc in range(CORES):
                if (o, oc) == (0, 0) or (o == 0 and not on_x):
                    continue
                pl.semaphore_signal(barrier, inc=1, device_id=peer(0, on_x, (pos + o) % size, (c + oc) % CORES),
                                    device_id_type=MESH)
                greeted += 1

    gain, bias = ng_ref[...].astype(F32), nb_ref[...].astype(F32)
    step = 2 * LANES
    spad = ch + PAD

    @pl.loop(0, rows)
    def _(i):
        yn = norm(z_ref[i], gain, bias, -1)
        yn_ref[i] = yn
        for kb in range(n // step):
            keep = mask_ref[pl.ds(i, 1), kb * step:(kb + 1) * step].astype(F32)
            ynk = yn[kb * step:(kb + 1) * step]
            for side, dst in ((0, sa_ref), (1, sb_ref)):
                w = wp_ref[side * 2 * ch:(side + 1) * 2 * ch]
                pr = dot(w, ynk, 1, 1)
                val = keep * jax.nn.sigmoid(pr[ch:]) * pr[:ch]
                for t in range(2):
                    dst[kb * 2 + t, pl.ds(pl.multiple_of(i * spad, 8), ch)] = val[:, t * LANES:(t + 1) * LANES]

    abf = ab_ref.reshape(2, ch, rows, n)

    @pl.loop(0, ch)
    def _(k):
        for side, src in ((0, sa_ref), (1, sb_ref)):
            for t in range(nt):
                abf[side, k, :, t * LANES:(t + 1) * LANES] = src[t, pl.ds(k, rows, stride=spad)].astype(BF16)

    pl.semaphore_wait(barrier, greeted)

    def send(src, dst, ss, rs, dev):
        cp = pltpu.make_async_remote_copy(src_ref=src, dst_ref=dst, send_sem=ss, recv_sem=rs, device_id=dev,
                                          device_id_type=MESH)
        cp.start()
        return cp

    sent = []
    hop1, hop2, back1, back2 = {}, {}, {}, {}
    rounds = [(r, s) for r in range(2) for s in range(2)]
    for r, s in rounds:
        hop1[r, s] = []
        for o in range(1, size1[s]):
            g = (pos1[s] + o) % size1[s]
            hop1[r, s].append(send(ab_ref.at[:, s, g, :, r], t_ref.at[s, :, :, r, pos1[s]], p1s.at[s, r, o],
                                   p1r.at[s, r, o], peer(s, True, g, c)))
    for r, s in rounds:
        t_ref[s, :, :, r, pos1[s]] = ab_ref[:, s, pos1[s], :, r]
    for r, s in rounds:
        for cp in hop1[r, s]:
            cp.wait_recv()
        hop2[r, s] = []
        for o in range(size2[s]):
            h = (pos2[s] + o) % size2[s]
            for oc in range(CORES):
                k = (c + oc) % CORES
                src = t_ref.at[s, :, h * CORES + k, r]
                dst = r_ref.at[:, s, r, y, :, c] if s == 0 else r_ref.at[:, s, r, :, x, c]
                if (o, oc) != (0, 0):
                    hop2[r, s].append(send(src, dst, p2s.at[s, r, o * CORES + oc], p2r.at[s, r, o * CORES + oc],
                                           peer(s, False, h, k)))
        own = t_ref[s, :, pos2[s] * CORES + c, r]
        if s == 0:
            r_ref[:, s, r, y, :, c] = own
        else:
            r_ref[:, s, r, :, x, c] = own
    blk = 2 * LANES
    rf = r_ref.reshape(2, 2, 2, n, n)
    xf = x_ref.reshape(2, 2, n // rows, nt * rows, LANES)
    for r, s in rounds:
        for cp in hop2[r, s]:
            cp.wait_recv()
        for ib in range(n // blk):
            for jb in range(n // blk):
                isl, jsl = slice(ib * blk, (ib + 1) * blk), slice(jb * blk, (jb + 1) * blk)
                if incoming:
                    prod = dot(rf[0, s, r, :, isl], rf[1, s, r, :, jsl], 0, 0)
                else:
                    prod = dot(rf[0, s, r, isl], rf[1, s, r, jsl], 1, 1)
                for t in range(2):
                    q = jb * 2 + t
                    xf[s, r, ib * (blk // rows):(ib + 1) * (blk // rows), q * rows:(q + 1) * rows, :] = (
                        prod[:, t * LANES:(t + 1) * LANES].reshape(blk // rows, rows, LANES))
        back1[r, s] = []
        for o in range(1, size2[s]):
            h = (pos2[s] + o) % size2[s]
            src = x_ref.at[s, r, h] if s == 0 else x_ref.at[s, r, :, h]
            back1[r, s].append(send(src, u_ref.at[s, :, :, pos2[s], r], x1s.at[s, r, o], x1r.at[s, r, o],
                                    peer(s, False, h, c)))
        u_ref[s, :, :, pos2[s], r] = x_ref[s, r, y] if s == 0 else x_ref[s, r, :, x]
    for r, s in rounds:
        for cp in back1[r, s]:
            cp.wait_recv()
        back2[r, s] = []
        for o in range(size1[s]):
            g = (pos1[s] + o) % size1[s]
            for oc in range(CORES):
                k = (c + oc) % CORES
                if (o, oc) != (0, 0):
                    back2[r, s].append(send(u_ref.at[s, g, k, :, r],
                                            xr_ref.at[s, pos1[s], :, c, r, pl.ds(0, nt * rows)],
                                            x2s.at[s, r, o * CORES + oc], x2r.at[s, r, o * CORES + oc],
                                            peer(s, True, g, k)))
        xr_ref[s, pos1[s], :, c, r, pl.ds(0, nt * rows)] = u_ref[s, pos1[s], c, :, r]
    for key in rounds:
        for cp in back2[key]:
            cp.wait_recv()

    pgain, pbias = pg_ref[...].astype(F32), pb_ref[...].astype(F32)
    xpad = nt * rows + PAD
    xrf = xr_ref.reshape(ch * xpad, LANES)

    @pl.loop(0, rows)
    def _(i):
        for t in range(nt):
            js = slice(t * LANES, (t + 1) * LANES)
            xn = norm(xrf[pl.ds(t * rows + i, ch, stride=xpad)], pgain, pbias, 0)
            upd = dot(xn, wo_ref[...], 0, 0)
            pre = dot(yn_ref[i, js], wg_ref[...], 1, 0)
            out_ref[i, js] = z_ref[i, js] + jax.nn.sigmoid(pre) * upd

    for group in (hop1, hop2, back1, back2):
        for key in rounds:
            for cp in group[key]:
                cp.wait_send()


def update(ny, nx, incoming, pair, mask, ng, nb, wp, wg, pg, pb, wo):
    rows, n, ch = pair.shape
    nt = n // LANES
    per = ch // (ny * nx * CORES * 2)
    assert per == 2 and ny == nx
    vmem = pl.BlockSpec(memory_space=pltpu.VMEM)
    dma = pltpu.SemaphoreType.DMA
    g = nx
    return pl.pallas_call(
        functools.partial(update_kernel, ny, nx, incoming),
        name='incoming' if incoming else 'outgoing',
        out_shape=jax.ShapeDtypeStruct(pair.shape, F32),
        in_specs=[vmem] * 9,
        out_specs=vmem,
        scratch_shapes=[
            pltpu.VMEM((rows, n, ch), BF16),
            pltpu.VMEM((nt, rows * (ch + PAD), LANES), F32),
            pltpu.VMEM((nt, rows * (ch + PAD), LANES), F32),
            pltpu.VMEM((2, 2, g, g * CORES, 2, rows, n), BF16),
            pltpu.VMEM((2, 2, g * CORES, 2, g, rows, n), BF16),
            pltpu.VMEM((2, 2, 2, ny, nx, CORES, rows, n), BF16),
            pltpu.VMEM((2, 2, ny, nx, CORES, nt * rows, LANES), F32),
            pltpu.VMEM((2, g, CORES, g, 2, nt * rows, LANES), F32),
            pltpu.VMEM((2, g, g, CORES, 2, nt * rows + PAD, LANES), F32),
            dma((2, 2, g)), dma((2, 2, g)), dma((2, 2, g * CORES)), dma((2, 2, g * CORES)),
            dma((2, 2, g)), dma((2, 2, g)), dma((2, 2, g * CORES)), dma((2, 2, g * CORES)),
        ],
        compiler_params=pltpu.CompilerParams(collective_id=1 if incoming else 0, has_side_effects=True,
                                             vmem_limit_bytes=60 * 2 ** 20),
    )(pair, mask, ng, nb, wp, wg, pg, pb, wo)


def solution(mesh):
    ny, nx = mesh.shape['dap2'], mesh.shape['dap'] // CORES

    def local_step(pair, mask, norm_gain, norm_bias, w_proj, w_gate, post_gain, post_bias, w_out):
        for s in range(2):
            pair = update(ny, nx, s == 1, pair, mask, norm_gain[s][None], norm_bias[s][None], w_proj[s].T, w_gate[s],
                          post_gain[s][:, None], post_bias[s][:, None], w_out[s])
        return pair

    return jax.shard_map(local_step, mesh=mesh, in_specs=(ROW_SPEC, MASK_SPEC) + (P(),) * 7, out_specs=ROW_SPEC,
                         check_vma=False)
```

time: 610 us -> 251 us (0.41)
  waiting for transfers between devices: 385 us -> 0 us
  Pallas kernels: 0 us -> 236 us
  matrix products: 138 us -> 0 us
  local copies, waits for them, and re-layouts: 39.3 us -> 14.3 us
  other arithmetic: 24 us -> 0 us
  between operations: 14.2 us -> 0.03 us
    all_gather x2 -> x0, waiting for transfers between devices: 340 us -> none  [local_step(): full_b = lax.all_gather(side_b, GROUP_AXES, axis=1, tiled=True)]
    pallas_call x0 -> x2, Pallas kernels: none -> 236 us  [update(): pl.pallas_call(functools.partial(update_kernel, ny, nx, incoming), name='...]
    dot_general x10 -> x0, matrix products: 138 us -> none  [the longest x1 61.1 us: local_step(): jnp.einsum('cki,ckj->cij', cols_a, full_b, preferred_element_type=jnp.flo...]
    all_to_all x1 -> x0, waiting for transfers between devices: 44.5 us -> none  [local_step(): cols_a = lax.all_to_all(side_a, GROUP_AXES, 2, 1, tiled=True)]
    convert_element_type x4 -> x0, local copies, waits for them, and re-layouts: 16.8 us -> none  [gated_side(): (keep_mask * jax.nn.sigmoid(projected[channels:]) * projected[:channels])...]
    convert_element_type x9 -> x0, other arithmetic: 12.5 us -> none  [the longest x2 7.65 us: gated_side(): (keep_mask * jax.nn.sigmoid(projected[channels:]) * projected[:channels])...]
    reduce_sum x5 -> x0, other arithmetic: 11.5 us -> none  [the longest x4 8.09 us: layer_norm(): row_var = jnp.mean(centered * centered, axis=norm_axis, keepdims=True)]
    all_to_all x2 -> x0, local copies, waits for them, and re-layouts: 7.38 us -> none  [local_step(): cols_a = lax.all_to_all(side_a, GROUP_AXES, 2, 1, tiled=True)]
  transfers between devices with their start and end apart: 3 -> 0, of which waited for: 3 -> 0; matrix products, arithmetic and copies ran while one was open for 4% -> 0% of each run, Pallas kernels for 0% -> 0%
where the time goes in v1:
time: 251 us
  Pallas kernels  236 us (94%)
  local copies, waits for them, and re-layouts  14.3 us (6%)
    pallas_call x2, Pallas kernels, update(): pl.pallas_call(functools.partial(update_kernel, ny, nx, incoming), name='...  236 us
    unnamed x3, local copies, waits for them, and re-layouts  6.12 us

profile of v1, /device:TPU:97, one launch (start us, length us, event | category | flops | bytes accessed | tf_op | source)
XLA Modules:
  0.0 250.8 jit_solution(7812294760843795293)
XLA Ops:
  0.0 0.7 slice_bitcast_fusion.5
  0.7 0.7 slice_bitcast_fusion.4
  1.5 1.3 fusion.1
  2.8 0.7 copy.15.pb_ref
  3.6 0.7 copy.14.pg_ref
  4.3 0.7 copy.12.pb_ref
  5.0 0.7 copy.11.pg_ref
  5.7 1.5 slice_bitcast_fusion
  7.2 1.0 fusion
  8.2 0.8 copy.17
  8.9 0.8 copy.16
  9.7 119.3 %outgoing.1.z_ref = f32[16,512,128]{2,1,0:T(8,128)} custom-call(f32[16,512,128]{2,1,0:T(8,128)} %z_ref.1, s32[16,512]{1,0:T(8,128)} %mask_ref.3, bf16[1,128]{1,0:T(2,128)(2,1)} %get-tuple-element.21.ng_ref, bf16[1,128]{1,0:T(2,128)(2,1)} %get-tuple-element.16.nb_ref, bf16[512,128]{1,0:T(8,128)(2,1)} %bitcast.23, bf16[128,128]{1,0:T(8,128)(2,1)} %get-tuple-element.19.wg_ref, ...), custom_call_target="tpu_custom_call" | custom-call | tf_op jit(solution)/shard_map/outgoing/pallas_call | solution.py:189
  129.0 117.2 %incoming.1 = f32[16,512,128]{2,1,0:T(8,128)} custom-call(f32[16,512,128]{2,1,0:T(8,128)} %outgoing.1.z_ref, s32[16,512]{1,0:T(8,128)} %mask_ref.3, bf16[1,128]{1,0:T(2,128)(2,1)} %get-tuple-element.22.ng_ref, bf16[1,128]{1,0:T(2,128)(2,1)} %get-tuple-element.15.nb_ref, bf16[512,128]{1,0:T(8,128)(2,1)} %bitcast.22, ...), custom_call_target="tpu_custom_call" | custom-call | tf_op jit(solution)/shard_map/incoming/pallas_call | solution.py:189
  246.1 4.6 %copy.19 = f32[16,512,128]{2,1,0:T(8,128)} copy(f32[16,512,128]{2,1,0:T(8,128)} %incoming.1) | data formatting | bytes 8388608

commit v2 on v0

v2 whole, which is shorter than its diff:
```python
import functools

import jax
import jax.numpy as jnp
from jax import lax
from jax.experimental import pallas as pl
from jax.experimental.pallas import tpu as pltpu
from jax.sharding import PartitionSpec as P

NORM_EPS = 1e-5
ROW_SPEC = P(('data', 'dap2', 'dap'), None, None)
MASK_SPEC = P(('data', 'dap2', 'dap'), None)
MESH = pl.DeviceIdType.MESH
F32, BF16 = jnp.float32, jnp.bfloat16
CORES = 2
LANES = 128
PAD = 8
HALVES = 2


def norm(values, gain, bias, axis):
    mean = jnp.mean(values, axis=axis, keepdims=True)
    centered = values - mean
    var = jnp.mean(centered * centered, axis=axis, keepdims=True)
    return (centered * lax.rsqrt(var + NORM_EPS) * gain + bias).astype(BF16)


def dot(a, b, ca, cb):
    return lax.dot_general(a, b, (((ca,), (cb,)), ((), ())), preferred_element_type=F32)


def both_updates(ny, nx, z_hbm, mask_ref, ng_ref, nb_ref, wp_ref, wg_ref, pg_ref, pb_ref, wo_ref, out_hbm,
                 z_ref, yn_ref, wt_ref, gb_ref, st_ref, ab_ref, t_ref, r_ref, x_ref, u_ref, xr_ref,
                 ssem, rsem, zsem):
    rows, n, ch = z_ref.shape
    width = n // HALVES
    nt = width // LANES
    xrows = nt * rows
    spad = ch + PAD
    xpad = HALVES * xrows + PAD
    y = lax.axis_index('dap2')
    d = lax.axis_index('dap')
    x, c = d // CORES, d % CORES
    size1, size2 = (nx, ny), (ny, nx)
    pos1, pos2 = (x, y), (y, x)
    blocks = ny * nx * CORES

    loads = []
    for q in range(HALVES):
        cols = pl.ds(q * width, width)
        loads.append(pltpu.make_async_copy(z_hbm.at[:, cols], z_ref.at[:, cols], zsem.at[0, q]))
        loads[q].start()

    def peer(s, first, place, core):
        on_x = (s == 0) == first
        return {'dap2': y, 'dap': place * CORES + core} if on_x else {'dap2': place, 'dap': x * CORES + core}

    barrier = pltpu.get_barrier_semaphore()
    greeted = 0
    for on_x, size, pos in ((True, nx, x), (False, ny, y)):
        for o in range(size):
            for oc in range(CORES):
                if (o, oc) == (0, 0) or (o == 0 and not on_x):
                    continue
                pl.semaphore_signal(barrier, inc=1, device_id=peer(0, on_x, (pos + o) % size, (c + oc) % CORES),
                                    device_id_type=MESH)
                greeted += 1

    for u in range(2):
        wt_ref[u] = wp_ref[u].T
        gb_ref[u, 0] = jnp.broadcast_to(pg_ref[u:u + 1].astype(F32), (LANES, ch)).T
        gb_ref[u, 1] = jnp.broadcast_to(pb_ref[u:u + 1].astype(F32), (LANES, ch)).T

    abf = ab_ref.reshape(2, ch, rows, n)
    rf = r_ref.reshape(2, 2, 2, 2, n, n)
    rw = r_ref.reshape(2, 2, 2, 2, blocks, rows, n)
    xf = x_ref.reshape(2, 2, blocks, HALVES * xrows, LANES)
    xrf = xr_ref.reshape(2 * ch * xpad, LANES)

    def finish_row(u, q, i):
        for t in range(nt):
            js = slice(q * width + t * LANES, q * width + (t + 1) * LANES)
            xn = norm(xrf[pl.ds(u * ch * xpad + (q * nt + t) * rows + i, ch, stride=xpad)], gb_ref[u, 0], gb_ref[u, 1], 0)
            upd = dot(xn, wo_ref[u], 0, 0)
            pre = dot(yn_ref[i, js], wg_ref[u], 1, 0)
            z_ref[i, js] = z_ref[i, js] + jax.nn.sigmoid(pre) * upd

    def project_row(u, q, i):
        js = slice(q * width, (q + 1) * width)
        yn = norm(z_ref[i, js], ng_ref[u:u + 1].astype(F32), nb_ref[u:u + 1].astype(F32), -1)
        yn_ref[i, js] = yn
        keep = mask_ref[pl.ds(i, 1), js].astype(F32)
        for side in range(2):
            pr = dot(wt_ref[u, side * 2 * ch:(side + 1) * 2 * ch], yn, 1, 1)
            val = keep * jax.nn.sigmoid(pr[ch:]) * pr[:ch]
            for t in range(nt):
                st_ref[side, t, pl.ds(pl.multiple_of(i * spad, 8), ch)] = val[:, t * LANES:(t + 1) * LANES]

    def repack(q):
        @pl.loop(0, ch)
        def _(k):
            for side in range(2):
                for t in range(nt):
                    lanes = slice(q * width + t * LANES, q * width + (t + 1) * LANES)
                    abf[side, k, :, lanes] = st_ref[side, t, pl.ds(k, rows, stride=spad)].astype(BF16)

    def send(src, dst, where, dev):
        pltpu.make_async_remote_copy(src_ref=src, dst_ref=dst, send_sem=ssem.at[where], recv_sem=rsem.at[where],
                                     device_id=dev, device_id_type=MESH).start()

    def wait(sem, view):
        pltpu.make_async_copy(view, view, sem).wait()

    HOP1, HOP2, BACK1, BACK2 = range(4)
    cols = [slice(q * width, (q + 1) * width) for q in range(HALVES)]
    xcols = [slice(q * xrows, (q + 1) * xrows) for q in range(HALVES)]

    def view(stage, u, q, r, s):
        if stage == HOP1:
            return t_ref.at[u, s, :, :, r, 0:size1[s] - 1, :, cols[q]]
        if stage == HOP2:
            return rw.at[u, :, s, r, 0:blocks - blocks // (size2[s] * CORES), :, cols[q]]
        if stage == BACK1:
            return xf.at[s, r, 0:blocks - blocks // size2[s], xcols[q]]
        return xf.at[s, r, 0:blocks - blocks // (size1[s] * CORES), xcols[q]]

    def arrived(stage, u, q, r):
        for s in range(2):
            wait(rsem.at[stage, u, q, r, s], view(stage, u, q, r, s))

    def left(stage, u):
        for q in range(HALVES):
            for r in range(2):
                for s in range(2):
                    wait(ssem.at[stage, u, q, r, s], view(stage, u, q, r, s))

    def hop1(u, q, r):
        for o in range(1, nx):
            for s in range(2):
                g = (pos1[s] + o) % size1[s]
                send(ab_ref.at[:, s, g, :, r, :, cols[q]], t_ref.at[u, s, :, :, r, pos1[s], :, cols[q]],
                     (HOP1, u, q, r, s), peer(s, True, g, c))
        for s in range(2):
            t_ref[u, s, :, :, r, pos1[s], :, cols[q]] = ab_ref[:, s, pos1[s], :, r, :, cols[q]]

    def hop2(u, q, r):
        arrived(HOP1, u, q, r)
        for o in range(ny):
            for oc in range(CORES):
                for s in range(2):
                    h, k = (pos2[s] + o) % size2[s], (c + oc) % CORES
                    src = (u, s, slice(None), h * CORES + k, r, slice(None), slice(None), cols[q])
                    dst = (u, slice(None), s, r) + ((y, slice(None)) if s == 0 else (slice(None), x)) + (
                        c, slice(None), cols[q])
                    if (o, oc) == (0, 0):
                        r_ref[dst] = t_ref[src]
                    else:
                        send(t_ref.at[src], r_ref.at[dst], (HOP2, u, q, r, s), peer(s, False, h, k))

    def product(u, r):
        blk = 2 * LANES
        for s in range(2):
            for ib in range(n // blk):
                for jb in range(n // blk):
                    isl, jsl = slice(ib * blk, (ib + 1) * blk), slice(jb * blk, (jb + 1) * blk)
                    if u == 1:
                        prod = dot(rf[u, 0, s, r, :, isl], rf[u, 1, s, r, :, jsl], 0, 0)
                    else:
                        prod = dot(rf[u, 0, s, r, isl], rf[u, 1, s, r, jsl], 1, 1)
                    per = blk // rows
                    for t in range(2):
                        w = jb * 2 + t
                        xf[s, r, ib * per:(ib + 1) * per, w * rows:(w + 1) * rows, :] = (
                            prod[:, t * LANES:(t + 1) * LANES].reshape(per, rows, LANES))

    def back1(u, q, r):
        for o in range(1, ny):
            for s in range(2):
                h = (pos2[s] + o) % size2[s]
                src = x_ref.at[s, r, h, :, :, xcols[q]] if s == 0 else x_ref.at[s, r, :, h, :, xcols[q]]
                send(src, u_ref.at[u, s, :, :, pos2[s], r, xcols[q]], (BACK1, u, q, r, s), peer(s, False, h, c))
        for s in range(2):
            u_ref[u, s, :, :, pos2[s], r, xcols[q]] = x_ref[s, r, y, :, :, xcols[q]] if s == 0 else (
                x_ref[s, r, :, x, :, xcols[q]])

    def back2(u, q, r):
        arrived(BACK1, u, q, r)
        for o in range(nx):
            for oc in range(CORES):
                for s in range(2):
                    g, k = (pos1[s] + o) % size1[s], (c + oc) % CORES
                    src, dst = (u, s, g, k, slice(None), r, xcols[q]), (u, s, pos1[s], slice(None), c, r, xcols[q])
                    if (o, oc) == (0, 0):
                        xr_ref[dst] = u_ref[src]
                    else:
                        send(u_ref.at[src], xr_ref.at[dst], (BACK2, u, q, r, s), peer(s, True, g, k))

    stores = []
    for u in range(3):
        for q in range(HALVES):
            if u > 0:
                for r in range(2):
                    arrived(BACK2, u - 1, q, r)
            else:
                loads[q].wait()
            if u == 1 and q == 0:
                left(HOP1, 0)

            @pl.loop(0, rows)
            def _(i):
                if u > 0:
                    finish_row(u - 1, q, i)
                if u < 2:
                    project_row(u, q, i)

            if u == 2:
                c_ = pl.ds(q * width, width)
                stores.append(pltpu.make_async_copy(z_ref.at[:, c_], out_hbm.at[:, c_], zsem.at[1, q]))
                stores[q].start()
                continue
            repack(q)
            if u == 0 and q == 0:
                pl.semaphore_wait(barrier, greeted)
            for r in range(2):
                hop1(u, q, r)
        if u == 2:
            break
        for q in range(HALVES):
            for r in range(2):
                hop2(u, q, r)
        if u == 1:
            left(BACK1, 0)
        for r in range(2):
            for q in range(HALVES):
                arrived(HOP2, u, q, r)
            product(u, r)
            back1(u, 0, r)
        for q in range(1, HALVES):
            for r in range(2):
                back1(u, q, r)
        for q in range(HALVES):
            for r in range(2):
                back2(u, q, r)
    for stage, u in ((HOP1, 1), (HOP2, 0), (HOP2, 1), (BACK1, 1), (BACK2, 0), (BACK2, 1)):
        left(stage, u)
    for q in range(HALVES):
        stores[q].wait()


def solution(mesh):
    ny, nx = mesh.shape['dap2'], mesh.shape['dap'] // CORES
    assert ny == nx
    g = nx

    def local_step(pair, mask, norm_gain, norm_bias, w_proj, w_gate, post_gain, post_bias, w_out):
        rows, n, ch = pair.shape
        nt = n // LANES
        assert ch == g * g * CORES * 4 and ch == LANES
        vmem = pl.BlockSpec(memory_space=pltpu.VMEM)
        hbm = pl.BlockSpec(memory_space=pl.ANY)
        dma = pltpu.SemaphoreType.DMA
        return pl.pallas_call(
            functools.partial(both_updates, ny, nx),
            name='triangle',
            out_shape=jax.ShapeDtypeStruct(pair.shape, F32),
            in_specs=[hbm] + [vmem] * 8,
            out_specs=hbm,
            scratch_shapes=[
                pltpu.VMEM((rows, n, ch), F32),
                pltpu.VMEM((rows, n, ch), BF16),
                pltpu.VMEM((2, 4 * ch, ch), BF16),
                pltpu.VMEM((2, 2, ch, LANES), F32),
                pltpu.VMEM((2, nt // HALVES, rows * (ch + PAD), LANES), F32),
                pltpu.VMEM((2, 2, g, g * CORES, 2, rows, n), BF16),
                pltpu.VMEM((2, 2, 2, g * CORES, 2, g, rows, n), BF16),
                pltpu.VMEM((2, 2, 2, 2, ny, nx, CORES, rows, n), BF16),
                pltpu.VMEM((2, 2, ny, nx, CORES, nt * rows, LANES), F32),
                pltpu.VMEM((2, 2, g, CORES, g, 2, nt * rows, LANES), F32),
                pltpu.VMEM((2, 2, g, g, CORES, 2, nt * rows + PAD, LANES), F32),
                dma((4, 2, HALVES, 2, 2)), dma((4, 2, HALVES, 2, 2)), dma((2, HALVES)),
            ],
            compiler_params=pltpu.CompilerParams(collective_id=0, has_side_effects=True,
                                                 vmem_limit_bytes=63 * 2 ** 20),
        )(pair, mask, norm_gain, norm_bias, w_proj, w_gate, post_gain, post_bias, w_out)

    return jax.shard_map(local_step, mesh=mesh, in_specs=(ROW_SPEC, MASK_SPEC) + (P(),) * 7, out_specs=ROW_SPEC,
                         check_vma=False)
```

time: 610 us -> 215 us (0.35)
  waiting for transfers between devices: 385 us -> 0 us
  Pallas kernels: 0 us -> 210 us
  matrix products: 138 us -> 0 us
  local copies, waits for them, and re-layouts: 39.3 us -> 4.61 us
  other arithmetic: 24 us -> 0 us
  between operations: 14.2 us -> 0.01 us
    all_gather x2 -> x0, waiting for transfers between devices: 340 us -> none  [local_step(): full_b = lax.all_gather(side_b, GROUP_AXES, axis=1, tiled=True)]
    pallas_call x0 -> x1, Pallas kernels: none -> 210 us  [local_step(): pl.pallas_call(functools.partial(both_updates, ny, nx), name='triangle',...]
    dot_general x10 -> x0, matrix products: 138 us -> none  [the longest x1 61.1 us: local_step(): jnp.einsum('cki,ckj->cij', cols_a, full_b, preferred_element_type=jnp.flo...]
    all_to_all x1 -> x0, waiting for transfers between devices: 44.5 us -> none  [local_step(): cols_a = lax.all_to_all(side_a, GROUP_AXES, 2, 1, tiled=True)]
    convert_element_type x4 -> x0, local copies, waits for them, and re-layouts: 16.8 us -> none  [gated_side(): (keep_mask * jax.nn.sigmoid(projected[channels:]) * projected[:channels])...]
    convert_element_type x9 -> x0, other arithmetic: 12.5 us -> none  [the longest x2 7.65 us: gated_side(): (keep_mask * jax.nn.sigmoid(projected[channels:]) * projected[:channels])...]
    reduce_sum x5 -> x0, other arithmetic: 11.5 us -> none  [the longest x4 8.09 us: layer_norm(): row_var = jnp.mean(centered * centered, axis=norm_axis, keepdims=True)]
    all_to_all x2 -> x0, local copies, waits for them, and re-layouts: 7.38 us -> none  [local_step(): cols_a = lax.all_to_all(side_a, GROUP_AXES, 2, 1, tiled=True)]
  transfers between devices with their start and end apart: 3 -> 0, of which waited for: 3 -> 0; matrix products, arithmetic and copies ran while one was open for 4% -> 0% of each run, Pallas kernels for 0% -> 0%
where the time goes in v2:
time: 215 us
  Pallas kernels  210 us (98%)
  local copies, waits for them, and re-layouts  4.61 us (2%)
    pallas_call x1, Pallas kernels, local_step(): pl.pallas_call(functools.partial(both_updates, ny, nx), name='triangle',...  210 us
    unnamed x1, local copies, waits for them, and re-layouts  4.61 us

profile of v2, /device:TPU:97, one launch (start us, length us, event | category | flops | bytes accessed | tf_op | source)
XLA Modules:
  0.0 215.0 jit_solution(1043328206651283852)
XLA Ops:
  0.0 210.4 %triangle.1 = f32[16,512,128]{2,1,0:T(8,128)} custom-call(f32[16,512,128]{2,1,0:T(8,128)} %z_hbm.1, s32[16,512]{1,0:T(8,128)} %mask_ref.1, bf16[2,128]{1,0:T(2,128)(2,1)} %ng_ref.1, bf16[2,128]{1,0:T(2,128)(2,1)} %nb_ref.1, bf16[2,128,512]{2,1,0:T(8,128)(2,1)} %wp_ref.1, bf16[2,128,128]{2,1,0:T(8,128)(2,1)} %wg_ref.1, bf16[2,128]{1,0:T(2,128)(2,1)} %pg_ref.1, ...), custom_call_target="tpu_custom_call" | custom-call | tf_op jit(solution)/shard_map/triangle/pallas_call | solution.py:262
  210.4 4.6 %copy.11 = f32[16,512,128]{2,1,0:T(8,128)} copy(f32[16,512,128]{2,1,0:T(8,128)} %triangle.1) | data formatting | bytes 8388608

commit v3 on v2

--- a/solution.py
+++ b/solution.py
@@ -16,6 +16,7 @@
 LANES = 128
 PAD = 8
 HALVES = 2
+RING = 4
 
 
 def norm(values, gain, bias, axis):
@@ -30,7 +31,7 @@
 
 
 def both_updates(ny, nx, z_hbm, mask_ref, ng_ref, nb_ref, wp_ref, wg_ref, pg_ref, pb_ref, wo_ref, out_hbm,
-                 z_ref, yn_ref, wt_ref, gb_ref, st_ref, ab_ref, t_ref, r_ref, x_ref, u_ref, xr_ref,
+                 z_ref, yn_ref, wt_ref, gb_ref, st_ref, ab_ref, a0_ref, b0_ref, t_ref, r_ref, x_ref, u_ref, xr_ref,
                  ssem, rsem, zsem):
     rows, n, ch = z_ref.shape
     width = n // HALVES
@@ -72,8 +73,16 @@
         gb_ref[u, 1] = jnp.broadcast_to(pb_ref[u:u + 1].astype(F32), (LANES, ch)).T
 
     abf = ab_ref.reshape(2, ch, rows, n)
-    rf = r_ref.reshape(2, 2, 2, 2, n, n)
-    rw = r_ref.reshape(2, 2, 2, 2, blocks, rows, n)
+    rf = r_ref.reshape(2, 2, 2, n, n)
+    rw = r_ref.reshape(2, 2, 2, blocks, rows, n)
+    band = nx * CORES
+    per0 = ch // (2 * band)
+    part = per0 // 2
+    ab0 = ab_ref.reshape(2, 2, nx, CORES, per0, rows, n)
+    a0f = a0_ref.reshape(2, per0, band * rows, n)
+    b0f = b0_ref.reshape(2, per0, n, n)
+    x0 = x_ref.reshape(2, per0, band, HALVES * xrows, LANES)
+    xr0 = xr_ref.reshape(2, 2, nx, CORES, per0, xpad, LANES)
     xf = x_ref.reshape(2, 2, blocks, HALVES * xrows, LANES)
     xrf = xr_ref.reshape(2 * ch * xpad, LANES)
 
@@ -97,7 +106,7 @@
                 st_ref[side, t, pl.ds(pl.multiple_of(i * spad, 8), ch)] = val[:, t * LANES:(t + 1) * LANES]
 
     def repack(q):
-        @pl.loop(0, ch)
+        @pl.loop(0, ch, unroll=8)
         def _(k):
             for side in range(2):
                 for t in range(nt):
@@ -116,10 +125,18 @@
     xcols = [slice(q * xrows, (q + 1) * xrows) for q in range(HALVES)]
 
     def view(stage, u, q, r, s):
+        if u == 0:
+            if stage == HOP1:
+                return abf.at[:, 0:(band - 1) * per0, :, cols[q]]
+            if stage == HOP2:
+                return b0_ref.at[s, :, 0, :, :, :, cols[q]]
+            if stage == BACK1:
+                return b0_ref.at[s, 0:part, 0, :, :, :, cols[q]]
+            return x0.at[s, 0:part, 0:band - 1, xcols[q]]
         if stage == HOP1:
-            return t_ref.at[u, s, :, :, r, 0:size1[s] - 1, :, cols[q]]
+            return t_ref.at[s, :, :, r, 0:size1[s] - 1, :, cols[q]]
         if stage == HOP2:
-            return rw.at[u, :, s, r, 0:blocks - blocks // (size2[s] * CORES), :, cols[q]]
+            return rw.at[:, s, r, 0:blocks - blocks // (size2[s] * CORES), :, cols[q]]
         if stage == BACK1:
             return xf.at[s, r, 0:blocks - blocks // size2[s], xcols[q]]
         return xf.at[s, r, 0:blocks - blocks // (size1[s] * CORES), xcols[q]]
@@ -130,70 +147,160 @@
 
     def left(stage, u):
         for q in range(HALVES):
-            for r in range(2):
+            for r in range(1 if (stage, u) == (HOP1, 0) else 2):
                 for s in range(2):
                     wait(ssem.at[stage, u, q, r, s], view(stage, u, q, r, s))
 
-    def hop1(u, q, r):
+    def slab(s, kk, h, q):
+        place = (h, slice(None)) if s == 0 else (slice(None), h)
+        return (s, kk) + place + (slice(None), slice(None), cols[q])
+
+    def spread(q):
+        for o in range(nx):
+            for oc in range(CORES):
+                for s in range(2):
+                    g, k = (pos1[s] + o) % size1[s], (c + oc) % CORES
+                    mine = pos1[s] * CORES + c
+                    for side, dst, at in ((1, b0_ref, (s, slice(None), y, x, c, slice(None), cols[q])),
+                                          (0, a0_ref, (s, slice(None), mine, slice(None), cols[q]))):
+                        src = (side, s, g, k, slice(None), slice(None), cols[q])
+                        if (o, oc) == (0, 0):
+                            dst[at] = ab0[src]
+                        else:
+                            send(ab0.at[src], dst.at[at], (HOP1, 0, q, 0, s), peer(s, True, g, k))
+
+    def gather(q, r):
+        for step in (1, -1):
+            for s in range(2):
+                at = slab(s, slice(r * part, (r + 1) * part), pos2[s], q)
+                send(b0_ref.at[at], b0_ref.at[at], (HOP2, 0, q, r, s), peer(s, False, (pos2[s] + step) % size2[s], c))
+
+    def relay(q, r):
+        arrived(HOP2, 0, q, r)
+        half = part // 2
+        for step, lo in ((1, 0), (-1, half)):
+            for s in range(2):
+                at = slab(s, slice(r * part + lo, r * part + lo + half), (pos2[s] - step) % size2[s], q)
+                send(b0_ref.at[at], b0_ref.at[at], (BACK1, 0, q, r, s), peer(s, False, (pos2[s] + step) % size2[s], c))
+
+    def product0(r):
+        for q in range(HALVES):
+            arrived(BACK1, 0, q, r)
+        blk = 2 * LANES
+        for s in range(2):
+            for k in range(r * part, (r + 1) * part):
+                for jb in range(n // blk):
+                    prod = dot(a0f[s, k], b0f[s, k, jb * blk:(jb + 1) * blk], 1, 1)
+                    for t in range(2):
+                        w = jb * 2 + t
+                        x0[s, k, :, w * rows:(w + 1) * rows, :] = (
+                            prod[:, t * LANES:(t + 1) * LANES].reshape(band, rows, LANES))
+
+    def give_back(q, r):
+        for o in range(nx):
+            for oc in range(CORES):
+                for s in range(2):
+                    g, k = (pos1[s] + o) % size1[s], (c + oc) % CORES
+                    kk = slice(r * part, (r + 1) * part)
+                    src, dst = (s, kk, g * CORES + k, xcols[q]), (0, s, pos1[s], c, kk, xcols[q])
+                    if (o, oc) == (0, 0):
+                        xr0[dst] = x0[src]
+                    else:
+                        send(x0.at[src], xr0.at[dst], (BACK2, 0, q, r, s), peer(s, True, g, k))
+
+    def outgoing():
+        for q in range(HALVES):
+            arrived(HOP1, 0, q, 0)
+            for r in range(2):
+                if (q, r) != (HALVES - 1, 1):
+                    gather(q, r)
+        for q in range(HALVES):
+            relay(q, 0)
+        gather(HALVES - 1, 1)
+        for q in range(HALVES - 1):
+            relay(q, 1)
+        product0(0)
+        relay(HALVES - 1, 1)
+        give_back(0, 0)
+        product0(1)
+        give_back(0, 1)
+        for q in range(1, HALVES):
+            for r in range(2):
+                give_back(q, r)
+
+    def hop1(q, r):
         for o in range(1, nx):
             for s in range(2):
                 g = (pos1[s] + o) % size1[s]
-                send(ab_ref.at[:, s, g, :, r, :, cols[q]], t_ref.at[u, s, :, :, r, pos1[s], :, cols[q]],
-                     (HOP1, u, q, r, s), peer(s, True, g, c))
-        for s in range(2):
-            t_ref[u, s, :, :, r, pos1[s], :, cols[q]] = ab_ref[:, s, pos1[s], :, r, :, cols[q]]
-
-    def hop2(u, q, r):
-        arrived(HOP1, u, q, r)
+                send(ab_ref.at[:, s, g, :, r, :, cols[q]], t_ref.at[s, :, :, r, pos1[s], :, cols[q]],
+                     (HOP1, 1, q, r, s), peer(s, True, g, c))
+        for s in range(2):
+            t_ref[s, :, :, r, pos1[s], :, cols[q]] = ab_ref[:, s, pos1[s], :, r, :, cols[q]]
+
+    def hop2(q, r):
+        arrived(HOP1, 1, q, r)
         for o in range(ny):
             for oc in range(CORES):
                 for s in range(2):
                     h, k = (pos2[s] + o) % size2[s], (c + oc) % CORES
-                    src = (u, s, slice(None), h * CORES + k, r, slice(None), slice(None), cols[q])
-                    dst = (u, slice(None), s, r) + ((y, slice(None)) if s == 0 else (slice(None), x)) + (
+                    src = (s, slice(None), h * CORES + k, r, slice(None), slice(None), cols[q])
+                    dst = (slice(None), s, r) + ((y, slice(None)) if s == 0 else (slice(None), x)) + (
                         c, slice(None), cols[q])
                     if (o, oc) == (0, 0):
                         r_ref[dst] = t_ref[src]
                     else:
-                        send(t_ref.at[src], r_ref.at[dst], (HOP2, u, q, r, s), peer(s, False, h, k))
-
-    def product(u, r):
+                        send(t_ref.at[src], r_ref.at[dst], (HOP2, 1, q, r, s), peer(s, False, h, k))
+
+    def product1(r):
+        for q in range(HALVES):
+            arrived(HOP2, 1, q, r)
         blk = 2 * LANES
+        per = blk // rows
         for s in range(2):
             for ib in range(n // blk):
                 for jb in range(n // blk):
-                    isl, jsl = slice(ib * blk, (ib + 1) * blk), slice(jb * blk, (jb + 1) * blk)
-                    if u == 1:
-                        prod = dot(rf[u, 0, s, r, :, isl], rf[u, 1, s, r, :, jsl], 0, 0)
-                    else:
-                        prod = dot(rf[u, 0, s, r, isl], rf[u, 1, s, r, jsl], 1, 1)
-                    per = blk // rows
+                    prod = dot(rf[0, s, r, :, ib * blk:(ib + 1) * blk], rf[1, s, r, :, jb * blk:(jb + 1) * blk], 0, 0)
                     for t in range(2):
                         w = jb * 2 + t
                         xf[s, r, ib * per:(ib + 1) * per, w * rows:(w + 1) * rows, :] = (
                             prod[:, t * LANES:(t + 1) * LANES].reshape(per, rows, LANES))
 
-    def back1(u, q, r):
+    def back1(q, r):
         for o in range(1, ny):
             for s in range(2):
                 h = (pos2[s] + o) % size2[s]
                 src = x_ref.at[s, r, h, :, :, xcols[q]] if s == 0 else x_ref.at[s, r, :, h, :, xcols[q]]
-                send(src, u_ref.at[u, s, :, :, pos2[s], r, xcols[q]], (BACK1, u, q, r, s), peer(s, False, h, c))
-        for s in range(2):
-            u_ref[u, s, :, :, pos2[s], r, xcols[q]] = x_ref[s, r, y, :, :, xcols[q]] if s == 0 else (
+                send(src, u_ref.at[s, :, :, pos2[s], r, xcols[q]], (BACK1, 1, q, r, s), peer(s, False, h, c))
+        for s in range(2):
+            u_ref[s, :, :, pos2[s], r, xcols[q]] = x_ref[s, r, y, :, :, xcols[q]] if s == 0 else (
                 x_ref[s, r, :, x, :, xcols[q]])
 
-    def back2(u, q, r):
-        arrived(BACK1, u, q, r)
+    def back2(q, r):
+        arrived(BACK1, 1, q, r)
         for o in range(nx):
             for oc in range(CORES):
                 for s in range(2):
                     g, k = (pos1[s] + o) % size1[s], (c + oc) % CORES
-                    src, dst = (u, s, g, k, slice(None), r, xcols[q]), (u, s, pos1[s], slice(None), c, r, xcols[q])
+                    src, dst = (s, g, k, slice(None), r, xcols[q]), (1, s, pos1[s], slice(None), c, r, xcols[q])
                     if (o, oc) == (0, 0):
                         xr_ref[dst] = u_ref[src]
                     else:
-                        send(u_ref.at[src], xr_ref.at[dst], (BACK2, u, q, r, s), peer(s, True, g, k))
+                        send(u_ref.at[src], xr_ref.at[dst], (BACK2, 1, q, r, s), peer(s, True, g, k))
+
+    def incoming():
+        for q in range(HALVES):
+            for r in range(2):
+                hop2(q, r)
+        left(BACK2, 0)
+        for r in range(2):
+            product1(r)
+            back1(0, r)
+        for q in range(1, HALVES):
+            for r in range(2):
+                back1(q, r)
+        for q in range(HALVES):
+            for r in range(2):
+                back2(q, r)
 
     stores = []
     for u in range(3):
@@ -206,7 +313,7 @@
             if u == 1 and q == 0:
                 left(HOP1, 0)
 
-            @pl.loop(0, rows)
+            @pl.loop(0, rows, unroll=4)
             def _(i):
                 if u > 0:
                     finish_row(u - 1, q, i)
@@ -221,27 +328,16 @@
             repack(q)
             if u == 0 and q == 0:
                 pl.semaphore_wait(barrier, greeted)
-            for r in range(2):
-                hop1(u, q, r)
-        if u == 2:
-            break
-        for q in range(HALVES):
-            for r in range(2):
-                hop2(u, q, r)
-        if u == 1:
-            left(BACK1, 0)
-        for r in range(2):
-            for q in range(HALVES):
-                arrived(HOP2, u, q, r)
-            product(u, r)
-            back1(u, 0, r)
-        for q in range(1, HALVES):
-            for r in range(2):
-                back1(u, q, r)
-        for q in range(HALVES):
-            for r in range(2):
-                back2(u, q, r)
-    for stage, u in ((HOP1, 1), (HOP2, 0), (HOP2, 1), (BACK1, 1), (BACK2, 0), (BACK2, 1)):
+            if u == 0:
+                spread(q)
+            else:
+                for r in range(2):
+                    hop1(q, r)
+        if u == 0:
+            outgoing()
+        elif u == 1:
+            incoming()
+    for stage, u in ((HOP1, 1), (HOP2, 0), (HOP2, 1), (BACK1, 0), (BACK1, 1), (BACK2, 1)):
         left(stage, u)
     for q in range(HALVES):
         stores[q].wait()
@@ -249,7 +345,7 @@
 
 def solution(mesh):
     ny, nx = mesh.shape['dap2'], mesh.shape['dap'] // CORES
-    assert ny == nx
+    assert ny == nx == RING
     g = nx
 
     def local_step(pair, mask, norm_gain, norm_bias, w_proj, w_gate, post_gain, post_bias, w_out):
@@ -272,10 +368,12 @@
                 pltpu.VMEM((2, 2, ch, LANES), F32),
                 pltpu.VMEM((2, nt // HALVES, rows * (ch + PAD), LANES), F32),
                 pltpu.VMEM((2, 2, g, g * CORES, 2, rows, n), BF16),
-                pltpu.VMEM((2, 2, 2, g * CORES, 2, g, rows, n), BF16),
-                pltpu.VMEM((2, 2, 2, 2, ny, nx, CORES, rows, n), BF16),
+                pltpu.VMEM((2, ch // (2 * g * CORES), g * CORES, rows, n), BF16),
+                pltpu.VMEM((2, ch // (2 * g * CORES), ny, nx, CORES, rows, n), BF16),
+                pltpu.VMEM((2, 2, g * CORES, 2, g, rows, n), BF16),
+                pltpu.VMEM((2, 2, 2, ny, nx, CORES, rows, n), BF16),
                 pltpu.VMEM((2, 2, ny, nx, CORES, nt * rows, LANES), F32),
-                pltpu.VMEM((2, 2, g, CORES, g, 2, nt * rows, LANES), F32),
+                pltpu.VMEM((2, g, CORES, g, 2, nt * rows, LANES), F32),
                 pltpu.VMEM((2, 2, g, g, CORES, 2, nt * rows + PAD, LANES), F32),
                 dma((4, 2, HALVES, 2, 2)), dma((4, 2, HALVES, 2, 2)), dma((2, HALVES)),
             ],

time: 215 us -> 194 us (0.902)
  Pallas kernels: 210 us -> 189 us
    pallas_call x1, Pallas kernels: 210 us -> 189 us  [local_step(): pl.pallas_call(functools.partial(both_updates, ny, nx), name='triangle',...]
where the time goes in v3:
time: 194 us
  Pallas kernels  189 us (97%)
  local copies, waits for them, and re-layouts  4.61 us (2%)
    pallas_call x1, Pallas kernels, local_step(): pl.pallas_call(functools.partial(both_updates, ny, nx), name='triangle',...  189 us
    unnamed x1, local copies, waits for them, and re-layouts  4.61 us

profile of v3, /device:TPU:97, one launch (start us, length us, event | category | flops | bytes accessed | tf_op | source)
XLA Modules:
  0.0 193.6 jit_solution(9086862508027827654)
XLA Ops:
  0.0 189.0 %triangle.1 = f32[16,512,128]{2,1,0:T(8,128)} custom-call(f32[16,512,128]{2,1,0:T(8,128)} %z_hbm.1, s32[16,512]{1,0:T(8,128)} %mask_ref.1, bf16[2,128]{1,0:T(2,128)(2,1)} %ng_ref.1, bf16[2,128]{1,0:T(2,128)(2,1)} %nb_ref.1, bf16[2,128,512]{2,1,0:T(8,128)(2,1)} %wp_ref.1, bf16[2,128,128]{2,1,0:T(8,128)(2,1)} %wg_ref.1, bf16[2,128]{1,0:T(2,128)(2,1)} %pg_ref.1, ...), custom_call_target="tpu_custom_call" | custom-call | tf_op jit(solution)/shard_map/triangle/pallas_call | solution.py:358
  189.0 4.6 %copy.11 = f32[16,512,128]{2,1,0:T(8,128)} copy(f32[16,512,128]{2,1,0:T(8,128)} %triangle.1) | data formatting | bytes 8388608

commit v4 on v3

--- a/solution.py
+++ b/solution.py
@@ -30,8 +30,8 @@
     return lax.dot_general(a, b, (((ca,), (cb,)), ((), ())), preferred_element_type=F32)
 
 
-def both_updates(ny, nx, z_hbm, mask_ref, ng_ref, nb_ref, wp_ref, wg_ref, pg_ref, pb_ref, wo_ref, out_hbm,
-                 z_ref, yn_ref, wt_ref, gb_ref, st_ref, ab_ref, a0_ref, b0_ref, t_ref, r_ref, x_ref, u_ref, xr_ref,
+def both_updates(ny, nx, z_hbm, mask_ref, ng_ref, nb_ref, wp_ref, wg_ref, pg_ref, pb_ref, wo_ref, z_ref,
+                 yn_ref, wt_ref, gb_ref, st_ref, ab_ref, a0_ref, b0_ref, t_ref, r_ref, x_ref, u_ref, xr_ref,
                  ssem, rsem, zsem):
     rows, n, ch = z_ref.shape
     width = n // HALVES
@@ -302,7 +302,6 @@
             for r in range(2):
                 back2(q, r)
 
-    stores = []
     for u in range(3):
         for q in range(HALVES):
             if u > 0:
@@ -321,9 +320,6 @@
                     project_row(u, q, i)
 
             if u == 2:
-                c_ = pl.ds(q * width, width)
-                stores.append(pltpu.make_async_copy(z_ref.at[:, c_], out_hbm.at[:, c_], zsem.at[1, q]))
-                stores[q].start()
                 continue
             repack(q)
             if u == 0 and q == 0:
@@ -339,8 +335,6 @@
             incoming()
     for stage, u in ((HOP1, 1), (HOP2, 0), (HOP2, 1), (BACK1, 0), (BACK1, 1), (BACK2, 1)):
         left(stage, u)
-    for q in range(HALVES):
-        stores[q].wait()
 
 
 def solution(mesh):
@@ -358,11 +352,10 @@
         return pl.pallas_call(
             functools.partial(both_updates, ny, nx),
             name='triangle',
-            out_shape=jax.ShapeDtypeStruct(pair.shape, F32),
+            out_shape=pltpu.VMEM(pair.shape, F32),
             in_specs=[hbm] + [vmem] * 8,
-            out_specs=hbm,
+            out_specs=vmem,
             scratch_shapes=[
-                pltpu.VMEM((rows, n, ch), F32),
                 pltpu.VMEM((rows, n, ch), BF16),
                 pltpu.VMEM((2, 4 * ch, ch), BF16),
                 pltpu.VMEM((2, 2, ch, LANES), F32),
@@ -375,10 +368,10 @@
                 pltpu.VMEM((2, 2, ny, nx, CORES, nt * rows, LANES), F32),
                 pltpu.VMEM((2, g, CORES, g, 2, nt * rows, LANES), F32),
                 pltpu.VMEM((2, 2, g, g, CORES, 2, nt * rows + PAD, LANES), F32),
-                dma((4, 2, HALVES, 2, 2)), dma((4, 2, HALVES, 2, 2)), dma((2, HALVES)),
+                dma((4, 2, HALVES, 2, 2)), dma((4, 2, HALVES, 2, 2)), dma((1, HALVES)),
             ],
             compiler_params=pltpu.CompilerParams(collective_id=0, has_side_effects=True,
-                                                 vmem_limit_bytes=63 * 2 ** 20),
+                                                 vmem_limit_bytes=56 * 2 ** 20),
         )(pair, mask, norm_gain, norm_bias, w_proj, w_gate, post_gain, post_bias, w_out)
 
     return jax.shard_map(local_step, mesh=mesh, in_specs=(ROW_SPEC, MASK_SPEC) + (P(),) * 7, out_specs=ROW_SPEC,

time: 194 us -> 190 us (0.979)
  local copies, waits for them, and re-layouts: 4.61 us -> 2.02 us
    unnamed x1, local copies, waits for them, and re-layouts: 4.61 us -> 2.02 us
where the time goes in v4:
time: 190 us
  Pallas kernels  188 us (99%)
  local copies, waits for them, and re-layouts  2.02 us (1%)
    pallas_call x1, Pallas kernels, local_step(): pl.pallas_call(functools.partial(both_updates, ny, nx), name='triangle',...  188 us

profile of v4, /device:TPU:97, one launch (start us, length us, event | category | flops | bytes accessed | tf_op | source)
XLA Modules:
  0.0 190.2 jit_solution(14145233727059146733)
XLA Ops:
  0.0 188.2 %triangle.1 = f32[16,512,128]{2,1,0:T(8,128)S(1)} custom-call(f32[16,512,128]{2,1,0:T(8,128)} %z_hbm.1, s32[16,512]{1,0:T(8,128)} %mask_ref.1, bf16[2,128]{1,0:T(2,128)(2,1)} %ng_ref.1, bf16[2,128]{1,0:T(2,128)(2,1)} %nb_ref.1, bf16[2,128,512]{2,1,0:T(8,128)(2,1)} %wp_ref.1, bf16[2,128,128]{2,1,0:T(8,128)(2,1)} %wg_ref.1, bf16[2,128]{1,0:T(2,128)(2,1)} %pg_ref.1, ...), custom_call_target="tpu_custom_call" | custom-call | tf_op jit(solution)/shard_map/triangle/pallas_call | solution.py:352
  188.2 2.0 %copy.11 = f32[16,512,128]{2,1,0:T(8,128)} copy(f32[16,512,128]{2,1,0:T(8,128)S(1)} %triangle.1) | data formatting | bytes 8388608
